TPU v7x, 32 devices: a whole 2x2x4 slice. The times are simulated.
32 devices in a mesh: ctx: 16 (over z, x, core), wa: 2 (over y).
Axes of the slice: x: 2, y: 2, z: 4, core: 2. Of those that a mesh axis runs over, the one named last changes fastest.
Arguments:
- tokens: bfloat16 [2, 6144, 768], P('wa', 'ctx'), may hold values from -6 to 6
- cotangent: bfloat16 [2, 6144, 768], P('wa', 'ctx'), may hold values from -6 to 6
- lengths: int32 [2, 3], P('wa'), may hold values from 1024 to 3072, as said below
- block_order: int32 [32], replicated, may hold values from 0 to 31, each once
- w_query: float32 [768, 768], P('wa'), may hold values from -0.21875 to 0.21875
- b_query: float32 [768], P('wa'), may hold values from -4 to 4
- w_key: float32 [768, 768], P('wa'), may hold values from -0.21875 to 0.21875
- w_value: float32 [768, 768], P('wa'), may hold values from -0.21875 to 0.21875
- b_value: float32 [768], P('wa'), may hold values from -4 to 4
- w_out: float32 [768, 768], P('wa'), may hold values from -6 to 6
- b_out: float32 [768], P('wa'), may hold values from -4 to 4
- gain_one: float32 [768], P('wa'), may hold values from 0.5 to 1.5
- shift_one: float32 [768], P('wa'), may hold values from -4 to 4
- w_up: float32 [768, 3072], P('wa'), may hold values from -0.21875 to 0.21875
- b_up: float32 [3072], P('wa'), may hold values from -4 to 4
- w_down: float32 [3072, 768], P('wa'), may hold values from -0.109375 to 0.109375
- b_down: float32 [768], P('wa'), may hold values from -4 to 4
- gain_two: float32 [768], P('wa'), may hold values from 0.5 to 1.5
- shift_two: float32 [768], P('wa'), may hold values from -4 to 4
Outputs:
- activations: bfloat16 [2, 6144, 768], P('wa', 'ctx')
- input_grad: bfloat16 [2, 6144, 768], P('wa', 'ctx')
- grad_w_query: float32 [768, 768], P('wa')
- grad_b_query: float32 [768], P('wa')
- grad_w_key: float32 [768, 768], P('wa')
- grad_w_value: float32 [768, 768], P('wa')
- grad_b_value: float32 [768], P('wa')
- grad_w_out: float32 [768, 768], P('wa')
- grad_b_out: float32 [768], P('wa')
- grad_gain_one: float32 [768], P('wa')
- grad_shift_one: float32 [768], P('wa')
- grad_w_up: float32 [768, 3072], P('wa')
- grad_b_up: float32 [3072], P('wa')
- grad_w_down: float32 [3072, 768], P('wa')
- grad_b_down: float32 [768], P('wa')
- grad_gain_two: float32 [768], P('wa')
- grad_shift_two: float32 [768], P('wa')
Inputs may be any that keep to these rules, and one draw needn't show every extreme that they name: `lengths`: each slot holds three sequences, each of 1024 tokens or more, one of them exactly 3072; the rest of the slot, 2 tokens or more, is padding. `block_order`: each block number appears once.
All inputs are finite; a program needn't handle non-finite values.
Results may differ from a plain program's by a relative error of at most 0.023.
Values may be sent and summed in bfloat16 or wider, within the bound.
A program may use at most 256 MiB of HBM per device.

v0:
```python
from functools import partial
import jax
import jax.numpy as jnp
from jax import lax
from jax.sharding import PartitionSpec as P

HEADS = 12
HEAD_DIM = 64
epsilon = 1e-05


def layer_norm(hidden, gain_vec, shift_vec):
    centre = hidden - jnp.mean(hidden, axis=-1, keepdims=True)
    spread = jnp.mean(centre * centre, axis=-1, keepdims=True)
    return centre * lax.rsqrt(spread + epsilon) * gain_vec + shift_vec


def segment_of(position, seq_ends):
    return jnp.sum((position[:, None] >= seq_ends[None, :]).astype(jnp.int32), axis=1)


def segment_ids(row_ids, block_order, seq_ends, half_len):
    dealt_slot = row_ids // (2 * half_len) * 2 + row_ids // half_len % 2
    table_ids = jnp.arange(block_order.shape[0], dtype=jnp.int32)
    block_ids = jnp.sum(
        jnp.where(dealt_slot[:, None] == table_ids[None, :], block_order[None, :], 0), axis=1
    )
    position = block_ids * half_len + row_ids % half_len
    return segment_of(position, seq_ends)


def block_steps(tok_rows):
    return 2 * tok_rows


def body(
    tokens,
    cotangent,
    lengths,
    block_order,
    w_query,
    b_query,
    w_key,
    w_value,
    b_value,
    w_out,
    b_out,
    gain_one,
    shift_one,
    w_up,
    b_up,
    w_down,
    b_down,
    gain_two,
    shift_two,
):
    low_type = jnp.bfloat16
    inputs = tokens[0]
    tok_rows = inputs.shape[0]
    width = inputs.shape[1]
    half_len = tok_rows // 2
    seq_ends = jnp.cumsum(lengths[0])
    own_rows = lax.axis_index("ctx") * tok_rows + jnp.arange(tok_rows, dtype=jnp.int32)
    own_seg = segment_ids(own_rows, block_order, seq_ends, half_len)
    (
        query_weight,
        query_bias,
        key_weight,
        value_weight,
        value_bias,
        out_weight,
        out_bias,
        gain_first,
        shift_first,
    ) = (
        lax.all_gather(w_query.astype(low_type), "wa", axis=0, tiled=True),
        lax.all_gather(b_query.astype(low_type), "wa", axis=0, tiled=True),
        lax.all_gather(w_key.astype(low_type), "wa", axis=0, tiled=True),
        lax.all_gather(w_value.astype(low_type), "wa", axis=0, tiled=True),
        lax.all_gather(b_value.astype(low_type), "wa", axis=0, tiled=True),
        lax.all_gather(w_out.astype(low_type), "wa", axis=0, tiled=True),
        lax.all_gather(b_out.astype(low_type), "wa", axis=0, tiled=True),
        lax.all_gather(gain_one.astype(low_type), "wa", axis=0, tiled=True),
        lax.all_gather(shift_one.astype(low_type), "wa", axis=0, tiled=True),
    )
    query_proj = (
        ((jnp.dot(inputs, query_weight, preferred_element_type=jnp.float32) + query_bias) * 0.125)
        .astype(low_type)
        .reshape(tok_rows, HEADS, HEAD_DIM)
    )
    key_proj = (
        jnp.dot(inputs, key_weight, preferred_element_type=jnp.float32)
        .astype(low_type)
        .reshape(tok_rows, HEADS, HEAD_DIM)
    )
    value_proj = (
        (jnp.dot(inputs, value_weight, preferred_element_type=jnp.float32) + value_bias)
        .astype(low_type)
        .reshape(tok_rows, HEADS, HEAD_DIM)
    )

    def key_segments(first_row, block_num, step_rows):
        rows_now = first_row + block_num * step_rows + jnp.arange(step_rows, dtype=jnp.int32)
        return segment_ids(rows_now, block_order, seq_ends, half_len)

    def forward_block(state, key_blk, value_blk, key_seg):
        acc_sum, total = state
        scores = jnp.einsum("qhd,khd->hqk", query_proj, key_blk, preferred_element_type=jnp.float32)
        mask = own_seg[:, None] == key_seg[None, :]
        expo = jnp.where(mask[None], jnp.exp(scores), 0.0)
        total = total + jnp.sum(expo, axis=-1)
        acc_sum = acc_sum + jnp.einsum(
            "hqk,khd->qhd", expo.astype(low_type), value_blk, preferred_element_type=jnp.float32
        )
        return (acc_sum, total)

    start_state = (
        jnp.zeros((tok_rows, HEADS, HEAD_DIM), jnp.float32),
        jnp.zeros((HEADS, tok_rows), jnp.float32),
    )
    key_whole, value_whole = (
        lax.all_gather(key_proj, "ctx", axis=0, tiled=True),
        lax.all_gather(value_proj, "ctx", axis=0, tiled=True),
    )
    row_count = key_whole.shape[0]
    step_rows = block_steps(tok_rows)
    count = row_count // step_rows
    stacked = (
        key_whole.reshape(count, step_rows, HEADS, HEAD_DIM),
        value_whole.reshape(count, step_rows, HEADS, HEAD_DIM),
        jnp.arange(count, dtype=jnp.int32),
    )

    def advance(carry_state, scan_item):
        key_blk, value_blk, block_num = scan_item
        key_seg = key_segments(0, block_num, step_rows)
        fresh = forward_block(carry_state, key_blk, value_blk, key_seg)
        return (fresh, None)

    final_state, _ = lax.scan(advance, start_state, stacked)
    acc_sum, total = final_state
    context = acc_sum / total.T[:, :, None]
    context_low = context.astype(low_type).reshape(tok_rows, width)
    up_weight, up_bias, down_weight, down_bias, gain_second, shift_second = (
        lax.all_gather(w_up.astype(low_type), "wa", axis=0, tiled=True),
        lax.all_gather(b_up.astype(low_type), "wa", axis=0, tiled=True),
        lax.all_gather(w_down.astype(low_type), "wa", axis=0, tiled=True),
        lax.all_gather(b_down.astype(low_type), "wa", axis=0, tiled=True),
        lax.all_gather(gain_two.astype(low_type), "wa", axis=0, tiled=True),
        lax.all_gather(shift_two.astype(low_type), "wa", axis=0, tiled=True),
    )
    attn_out = jnp.dot(context_low, out_weight, preferred_element_type=jnp.float32) + out_bias
    h_one = inputs.astype(jnp.float32) + attn_out
    norm_one, norm_one_back = jax.vjp(
        layer_norm, h_one, gain_first.astype(jnp.float32), shift_first.astype(jnp.float32)
    )
    norm_low = norm_one.astype(low_type)
    up_pre = jnp.dot(norm_low, up_weight, preferred_element_type=jnp.float32) + up_bias
    gelu_out, gelu_back = jax.vjp(partial(jax.nn.gelu, approximate=False), up_pre)
    gelu_low = gelu_out.astype(low_type)
    down_out = jnp.dot(gelu_low, down_weight, preferred_element_type=jnp.float32) + down_bias
    h_two = norm_one + down_out
    result, norm_two_back = jax.vjp(
        layer_norm, h_two, gain_second.astype(jnp.float32), shift_second.astype(jnp.float32)
    )
    activations = result.astype(low_type)[None]
    valid = (own_seg < 3).astype(jnp.float32)
    g_out = cotangent[0].astype(jnp.float32) * valid[:, None]
    d_htwo, grad_gain_second, grad_shift_second = norm_two_back(g_out)
    d_down = d_htwo.astype(low_type)
    grad_wdown = jnp.einsum("tf,td->fd", gelu_low, d_down, preferred_element_type=jnp.float32)
    grad_bdown = jnp.sum(d_down.astype(jnp.float32), axis=0)
    d_gelu = jnp.einsum("td,fd->tf", d_down, down_weight, preferred_element_type=jnp.float32)
    (d_uppre,) = gelu_back(d_gelu)
    d_up = d_uppre.astype(low_type)
    grad_wup = jnp.einsum("td,tf->df", norm_low, d_up, preferred_element_type=jnp.float32)
    grad_bup = jnp.sum(d_up.astype(jnp.float32), axis=0)
    d_yone = d_htwo + jnp.einsum("tf,df->td", d_up, up_weight, preferred_element_type=jnp.float32)
    d_hone, grad_gain_first, grad_shift_first = norm_one_back(d_yone)
    d_attn = d_hone.astype(low_type)
    grad_wout = jnp.einsum("tc,td->cd", context_low, d_attn, preferred_element_type=jnp.float32)
    grad_bout = jnp.sum(d_attn.astype(jnp.float32), axis=0)
    d_context = jnp.einsum(
        "td,cd->tc", d_attn, out_weight, preferred_element_type=jnp.float32
    ).reshape(tok_rows, HEADS, HEAD_DIM)
    d_acc = (d_context / total.T[:, :, None]).astype(low_type)
    d_total = -jnp.sum(d_context * context, axis=-1).T / total

    def block_scores(key_blk, value_blk, key_seg):
        scores = jnp.einsum("qhd,khd->hqk", query_proj, key_blk, preferred_element_type=jnp.float32)
        mask = own_seg[:, None] == key_seg[None, :]
        expo = jnp.where(mask[None], jnp.exp(scores), 0.0)
        d_prob = jnp.einsum("qhd,khd->hqk", d_acc, value_blk, preferred_element_type=jnp.float32)
        d_scores = (expo * (d_prob + d_total[:, :, None])).astype(low_type)
        return (expo, d_scores)

    def backward_block(dq_sum, key_blk, value_blk, key_seg):
        expo, d_scores = block_scores(key_blk, value_blk, key_seg)
        dq_sum = dq_sum + jnp.einsum(
            "hqk,khd->qhd", d_scores, key_blk, preferred_element_type=jnp.float32
        )
        d_keyblk = jnp.einsum(
            "hqk,qhd->khd", d_scores, query_proj, preferred_element_type=jnp.float32
        )
        d_valueblk = jnp.einsum(
            "hqk,qhd->khd", expo.astype(low_type), d_acc, preferred_element_type=jnp.float32
        )
        return (dq_sum, (d_keyblk, d_valueblk))

    whole_rows = key_whole.shape[0]
    back_rows = 2 * tok_rows
    back_count = whole_rows // back_rows
    back_stack = (
        key_whole.reshape(back_count, back_rows, HEADS, HEAD_DIM),
        value_whole.reshape(back_count, back_rows, HEADS, HEAD_DIM),
        jnp.arange(back_count, dtype=jnp.int32),
    )
    dq_start = jnp.zeros((tok_rows, HEADS, HEAD_DIM), jnp.float32)

    def retreat(dq_sum, scan_item):
        key_blk, value_blk, block_num = scan_item
        key_seg = key_segments(0, block_num, back_rows)
        return backward_block(dq_sum, key_blk, value_blk, key_seg)

    dq_sum, (key_terms, value_terms) = lax.scan(retreat, dq_start, back_stack)
    key_terms = key_terms.reshape(whole_rows, HEADS, HEAD_DIM)
    value_terms = value_terms.reshape(whole_rows, HEADS, HEAD_DIM)
    key_sum, value_sum = (
        lax.psum_scatter(
            key_terms.astype(jnp.bfloat16), "ctx", scatter_dimension=0, tiled=True
        ).astype(jnp.float32),
        lax.psum_scatter(
            value_terms.astype(jnp.bfloat16), "ctx", scatter_dimension=0, tiled=True
        ).astype(jnp.float32),
    )
    d_keys = key_sum.astype(low_type).reshape(tok_rows, width)
    d_values = value_sum.astype(low_type).reshape(tok_rows, width)
    d_queries = (
        (dq_sum.astype(low_type).astype(jnp.float32) * 0.125)
        .astype(low_type)
        .reshape(tok_rows, width)
    )
    grad_wquery = jnp.einsum("tc,td->cd", inputs, d_queries, preferred_element_type=jnp.float32)
    grad_bquery = jnp.sum(d_queries.astype(jnp.float32), axis=0)
    grad_wkey = jnp.einsum("tc,td->cd", inputs, d_keys, preferred_element_type=jnp.float32)
    grad_wvalue = jnp.einsum("tc,td->cd", inputs, d_values, preferred_element_type=jnp.float32)
    grad_bvalue = jnp.sum(d_values.astype(jnp.float32), axis=0)
    d_input = d_hone + jnp.einsum(
        "td,cd->tc", d_queries, query_weight, preferred_element_type=jnp.float32
    )
    d_input = d_input + jnp.einsum(
        "td,cd->tc", d_keys, key_weight, preferred_element_type=jnp.float32
    )
    d_input = d_input + jnp.einsum(
        "td,cd->tc", d_values, value_weight, preferred_element_type=jnp.float32
    )
    input_grad = d_input.astype(low_type)[None]
    shards = (
        lax.psum_scatter(
            grad_wquery.astype(jnp.bfloat16), "wa", scatter_dimension=0, tiled=True
        ).astype(jnp.float32),
        lax.psum_scatter(
            grad_bquery.astype(jnp.bfloat16), "wa", scatter_dimension=0, tiled=True
        ).astype(jnp.float32),
        lax.psum_scatter(
            grad_wkey.astype(jnp.bfloat16), "wa", scatter_dimension=0, tiled=True
        ).astype(jnp.float32),
        lax.psum_scatter(
            grad_wvalue.astype(jnp.bfloat16), "wa", scatter_dimension=0, tiled=True
        ).astype(jnp.float32),
        lax.psum_scatter(
            grad_bvalue.astype(jnp.bfloat16), "wa", scatter_dimension=0, tiled=True
        ).astype(jnp.float32),
        lax.psum_scatter(
            grad_wout.astype(jnp.bfloat16), "wa", scatter_dimension=0, tiled=True
        ).astype(jnp.float32),
        lax.psum_scatter(
            grad_bout.astype(jnp.bfloat16), "wa", scatter_dimension=0, tiled=True
        ).astype(jnp.float32),
        lax.psum_scatter(
            grad_gain_first.astype(jnp.bfloat16), "wa", scatter_dimension=0, tiled=True
        ).astype(jnp.float32),
        lax.psum_scatter(
            grad_shift_first.astype(jnp.bfloat16), "wa", scatter_dimension=0, tiled=True
        ).astype(jnp.float32),
        lax.psum_scatter(
            grad_wup.astype(jnp.bfloat16), "wa", scatter_dimension=0, tiled=True
        ).astype(jnp.float32),
        lax.psum_scatter(
            grad_bup.astype(jnp.bfloat16), "wa", scatter_dimension=0, tiled=True
        ).astype(jnp.float32),
        lax.psum_scatter(
            grad_wdown.astype(jnp.bfloat16), "wa", scatter_dimension=0, tiled=True
        ).astype(jnp.float32),
        lax.psum_scatter(
            grad_bdown.astype(jnp.bfloat16), "wa", scatter_dimension=0, tiled=True
        ).astype(jnp.float32),
        lax.psum_scatter(
            grad_gain_second.astype(jnp.bfloat16), "wa", scatter_dimension=0, tiled=True
        ).astype(jnp.float32),
        lax.psum_scatter(
            grad_shift_second.astype(jnp.bfloat16), "wa", scatter_dimension=0, tiled=True
        ).astype(jnp.float32),
    )
    summed = (
        lax.psum(shards[0].astype(jnp.bfloat16), "ctx").astype(jnp.float32),
        lax.psum(shards[1].astype(jnp.bfloat16), "ctx").astype(jnp.float32),
        lax.psum(shards[2].astype(jnp.bfloat16), "ctx").astype(jnp.float32),
        lax.psum(shards[3].astype(jnp.bfloat16), "ctx").astype(jnp.float32),
        lax.psum(shards[4].astype(jnp.bfloat16), "ctx").astype(jnp.float32),
        lax.psum(shards[5].astype(jnp.bfloat16), "ctx").astype(jnp.float32),
        lax.psum(shards[6].astype(jnp.bfloat16), "ctx").astype(jnp.float32),
        lax.psum(shards[7].astype(jnp.bfloat16), "ctx").astype(jnp.float32),
        lax.psum(shards[8].astype(jnp.bfloat16), "ctx").astype(jnp.float32),
        lax.psum(shards[9].astype(jnp.bfloat16), "ctx").astype(jnp.float32),
        lax.psum(shards[10].astype(jnp.bfloat16), "ctx").astype(jnp.float32),
        lax.psum(shards[11].astype(jnp.bfloat16), "ctx").astype(jnp.float32),
        lax.psum(shards[12].astype(jnp.bfloat16), "ctx").astype(jnp.float32),
        lax.psum(shards[13].astype(jnp.bfloat16), "ctx").astype(jnp.float32),
        lax.psum(shards[14].astype(jnp.bfloat16), "ctx").astype(jnp.float32),
    )
    return (
        activations,
        input_grad,
        summed[0],
        summed[1],
        summed[2],
        summed[3],
        summed[4],
        summed[5],
        summed[6],
        summed[7],
        summed[8],
        summed[9],
        summed[10],
        summed[11],
        summed[12],
        summed[13],
        summed[14],
    )


def solution(mesh):
    placed = (
        P("wa", "ctx", None),
        P("wa", "ctx", None),
        P("wa", None),
        P(),
        P("wa", None),
        P("wa"),
        P("wa", None),
        P("wa", None),
        P("wa"),
        P("wa", None),
        P("wa"),
        P("wa"),
        P("wa"),
        P("wa", None),
        P("wa"),
        P("wa", None),
        P("wa"),
        P("wa"),
        P("wa"),
    )
    return jax.shard_map(
        body,
        mesh=mesh,
        in_specs=placed,
        out_specs=(
            P("wa", "ctx", None),
            P("wa", "ctx", None),
            P("wa", None),
            P("wa"),
            P("wa", None),
            P("wa", None),
            P("wa"),
            P("wa", None),
            P("wa"),
            P("wa"),
            P("wa"),
            P("wa", None),
            P("wa"),
            P("wa", None),
            P("wa"),
            P("wa"),
            P("wa"),
        ),
        check_vma=False,
    )
```

profile of v0, /device:TPU:0, one launch (start us, length us, event | category | flops | bytes accessed | tf_op | source)
XLA Modules:
  0.0 1424.4 jit_solution(14266771286409439732)
XLA Ops:
  16.9 18.7 %all-gather.18.cloned.1.call-done = bf16[768,768]{1,0:T(8,128)(2,1)} async-done(((bf16[384,768]{1,0:T(8,128)(2,1)}), bf16[768,768]{1,0:T(8,128)(2,1)}) %all-gather.18.cloned.1.call-update) | async-done | bytes 1179664 | tf_op jit(solution)/shard_map/all_gather | solution.py:79
  38.7 21.9 %all-gather.22.cloned.1.call-done = bf16[768,768]{1,0:T(8,128)(2,1)} async-done(((bf16[384,768]{1,0:T(8,128)(2,1)}), bf16[768,768]{1,0:T(8,128)(2,1)}) %all-gather.22.cloned.1.call-update) | async-done | bytes 1179664 | tf_op jit(solution)/shard_map/all_gather | solution.py:78
  111.9 60.1 %all-gather.20.cloned.1.call-done = bf16[6144,12,64]{0,2,1:T(8,128)(2,1)} async-done(((bf16[384,12,64]{0,2,1:T(8,128)(2,1)}), bf16[6144,12,64]{0,2,1:T(8,128)(2,1)}) %all-gather.20.cloned.1.call-update) | async-done | bytes 9437200 | tf_op jit(solution)/shard_map/all_gather | solution.py:123
  172.1 8.5 copy.124
  180.6 76.2 %all-gather.24.cloned.1.call-done = bf16[6144,12,64]{0,2,1:T(8,128)(2,1)} async-done(((bf16[384,12,64]{0,2,1:T(8,128)(2,1)}), bf16[6144,12,64]{0,2,1:T(8,128)(2,1)}) %all-gather.24.cloned.1.call-update) | async-done | bytes 9437200 | tf_op jit(solution)/shard_map/all_gather | solution.py:122
  256.8 8.7 copy.123
  265.5 153.1 %while.34 = (s32[]{:T(128)}, f32[384,12,64]{0,2,1:T(8,128)S(1)}, f32[12,384]{1,0:T(8,128)S(1)}, bf16[8,768,12,64]{1,3,2,0:T(8,128)(2,1)}, s32[384]{0:T(512)S(1)}...) while((s32[]{:T(128)}, f32[384,12,64]{0,2,1:T(8,128)S(1)}, ...), condition=%wide.region_7.8_spmd.clone, body=%wide.region_3.7_spmd.clone.sunk | while | flops 921122304 | bytes 34605872 | solution.py:140
  267.4 9.0 fusion.174
  286.1 9.9 fusion.174
  305.8 9.0 fusion.174
  324.6 9.0 fusion.174
  343.4 9.2 fusion.174
  352.6 9.7 fusion.175
  364.0 9.0 fusion.174
  373.0 8.1 fusion.175
  382.7 9.0 fusion.174
  401.5 9.0 fusion.174
  422.2 15.7 %multiply_convert_fusion = (bf16[384,3072]{1,0:T(8,128)(2,1)}, f32[384,3072]{1,0:T(8,128)}, f32[384,3072]{1,0:T(8,128)}) fusion(f32[3072]{0:T(1024)S(1)} %bitcast.223, bf16[768,3072]{1,0:T(8,128)(2,1)} %all-gather.30.cloned.1.call-done, f32[384,768]{1,0:T(8,128)S(1)} %get-tuple-element.736, f32[768]{0:T(1024)S(1)} %reshape.392, f32[768]{0:T(1024)S(1)} %reshape.391, ...), kind=kOutput, calls=%fused_computation.90 | convolution fusion | flops 1891270656 | bytes 17716224 | tf_op jit(solution)/shard_map/dot_general | solution.py:158
  460.1 282.4 %while.35 = (s32[]{:T(128)}, f32[384,12,64]{0,2,1:T(8,128)}, bf16[8,768,12,64]{1,3,2,0:T(8,128)(2,1)}, bf16[8,768,12,64]{1,3,2,0:T(8,128)(2,1)}, bf16[8,768,12,6...) while((s32[]{:T(128)}, f32[384,12,64]{0,2,1:T(8,128)}, ...), condition=%wide.region_20.21_spmd.clone, body=%wide.region_17.20_spmd.clone.sunk | while | flops 2287150080 | bytes 150747632 | solution.py:225
  465.7 9.2 fusion.189
  481.5 8.6 bitcast_dynamic-update-slice_fusion.5
  501.0 9.2 fusion.189
  516.7 8.5 bitcast_dynamic-update-slice_fusion.5
  536.2 9.2 fusion.189
  551.9 8.6 bitcast_dynamic-update-slice_fusion.5
  571.4 9.2 fusion.189
  587.2 8.5 bitcast_dynamic-update-slice_fusion.5
  606.7 9.2 fusion.189
  622.4 8.6 bitcast_dynamic-update-slice_fusion.5
  642.0 9.2 fusion.189
  657.6 8.6 bitcast_dynamic-update-slice_fusion.5
  677.2 9.2 fusion.189
  692.9 8.6 bitcast_dynamic-update-slice_fusion.5
  712.4 9.2 fusion.189
  728.2 8.5 bitcast_dynamic-update-slice_fusion.5
  742.6 28.1 %copy.113 = bf16[8,768,12,64]{3,2,1,0:T(8,128)(2,1)} copy(bf16[8,768,12,64]{1,3,2,0:T(8,128)(2,1)} %get-tuple-element.403) | data formatting | bytes 18874368
  770.7 30.0 %reshape.397 = bf16[6144,768]{1,0:T(8,128)(2,1)} reshape(bf16[6144,12,64]{2,1,0:T(8,128)(2,1)} %bitcast.205) | data formatting | bytes 18874368
  800.8 28.8 %copy.115 = bf16[8,768,12,64]{3,2,1,0:T(8,128)(2,1)} copy(bf16[8,768,12,64]{1,3,2,0:T(8,128)(2,1)} %get-tuple-element.404) | data formatting | bytes 18874368
  829.6 30.3 %reshape.399 = bf16[6144,768]{1,0:T(8,128)(2,1)} reshape(bf16[6144,12,64]{2,1,0:T(8,128)(2,1)} %bitcast.206) | data formatting | bytes 18874368
  863.7 47.4 %reduce-scatter.25.cloned.1.call-done = bf16[384,768]{1,0:T(8,128)(2,1)} async-done(((bf16[6144,768]{1,0:T(8,128)(2,1)}), bf16[384,768]{1,0:T(8,128)(2,1)}) %reduce-scatter.25.cloned.1.call-update) | async-done | bytes 589840 | tf_op jit(solution)/shard_map/reshape | solution.py:236
  914.4 111.4 %reduce-scatter.27.cloned.1.call-done = bf16[384,768]{1,0:T(8,128)(2,1)} async-done(((bf16[6144,768]{1,0:T(8,128)(2,1)}), bf16[384,768]{1,0:T(8,128)(2,1)}) %reduce-scatter.27.cloned.1.call-update) | async-done | bytes 589840 | tf_op jit(solution)/shard_map/reshape | solution.py:237
  1052.3 22.4 %reduce-scatter.31.cloned.1.call-done = bf16[384,768]{1,0:T(8,128)(2,1)} async-done(((bf16[768,768]{1,0:T(8,128)(2,1)}), bf16[384,768]{1,0:T(8,128)(2,1)}) %reduce-scatter.31.cloned.1.call-update) | async-done | bytes 589840
  1076.8 22.6 %reduce-scatter.33.cloned.1.call-done = bf16[384,768]{1,0:T(8,128)(2,1)} async-done(((bf16[768,768]{1,0:T(8,128)(2,1)}), bf16[384,768]{1,0:T(8,128)(2,1)}) %reduce-scatter.33.cloned.1.call-update) | async-done | bytes 589840
  1101.5 21.9 %reduce-scatter.19.cloned.1.call-done = bf16[384,768]{1,0:T(8,128)(2,1)} async-done(((bf16[768,768]{1,0:T(8,128)(2,1)}), bf16[384,768]{1,0:T(8,128)(2,1)}) %reduce-scatter.19.cloned.1.call-update) | async-done | bytes 589840 | tf_op jit(solution)/shard_map/reduce_scatter | solution.py:274
  1123.4 62.8 %reduce-scatter.21.cloned.1.call-done = bf16[384,3072]{1,0:T(8,128)(2,1)} async-done(((bf16[768,3072]{1,0:T(8,128)(2,1)}), bf16[384,3072]{1,0:T(8,128)(2,1)}) %reduce-scatter.21.cloned.1.call-update) | async-done | bytes 2359312 | tf_op jit(solution)/shard_map/reduce_scatter | solution.py:286
  1186.2 62.8 %reduce-scatter.23.cloned.1.call-done = bf16[1536,768]{1,0:T(8,128)(2,1)} async-done(((bf16[3072,768]{1,0:T(8,128)(2,1)}), bf16[1536,768]{1,0:T(8,128)(2,1)}) %reduce-scatter.23.cloned.1.call-update) | async-done | bytes 2359312 | tf_op jit(solution)/shard_map/reduce_scatter | solution.py:292
  1263.5 62.2 %all-reduce.9 = (bf16[384]{0:T(512)(128)(2,1)S(1)}, bf16[384]{0:T(512)(128)(2,1)S(1)}, bf16[384]{0:T(512)(128)(2,1)S(1)}, bf16[384]{0:T(512)(128)(2,1)S(1)}, bf1...) all-reduce(bf16[384]{0:T(512)(128)(2,1)S(1)} %dynamic-slice.1, ...), channel_id=1, replica_groups=mesh['ctx'=16,'wa'=2] {'ctx'}, use_global_device_ids=true, to_apply=%region_27.28 | all-reduce | flops 4608 | bytes 18432 | tf_op jit(solution)/shard_map/psum | solution.py:307
  1334.5 71.0 %all-reduce.14.cloned.1.call-done = (bf16[384,768]{0,1:T(8,128)(2,1)}, bf16[384,768]{0,1:T(8,128)(2,1)}, bf16[384,768]{0,1:T(8,128)(2,1)}, bf16[384,768]{1,0:T(8...) async-done(((bf16[384,768]{0,1:T(8,128)(2,1)}, bf16[384,768]{0,1:T(8,128)(2,1)}, bf16[384,768]{0,1:T(8,128)(2,1)}, bf16[384,768]{1,0:T(8,128)(2,1)}, ...) | async-done | bytes 7077904 | tf_op jit(solution)/shard_map/psum | solution.py:306
  (516 shorter events, 352.3 us)
Async XLA Ops:
  7.2 28.4 %all-gather.18.cloned.1.call-start = ((), (), s32[]{:S(2)}) async-start(), calls=%async_computation.8 | async-start | bytes 1769472 | tf_op jit(solution)/shard_map/all_gather | solution.py:79
  9.6 26.1 %copy-start.28 = (bf16[1,384,768]{2,1,0:T(8,128)(2,1)S(1)}, bf16[1,384,768]{2,1,0:T(8,128)(2,1)}, u32[]{:S(2)}) copy-start(bf16[1,384,768]{2,1,0:T(8,128)(2,1)} %param.23) | copy-start | bytes 1769476
  9.6 51.0 %all-gather.22.cloned.1.call-start = ((), (), s32[]{:S(2)}) async-start(), calls=%async_computation.10 | async-start | bytes 1769472 | tf_op jit(solution)/shard_map/all_gather | solution.py:78
  10.6 99.2 %all-gather.26.cloned.1.call-start = ((), (), s32[]{:S(2)}) async-start(), calls=%async_computation.12 | async-start | bytes 1769472 | tf_op jit(solution)/shard_map/all_gather | solution.py:76
  11.5 160.6 %all-gather.20.cloned.1.call-start = ((), (), s32[]{:S(2)}) async-start(), calls=%async_computation.9 | async-start | bytes 10027008 | tf_op jit(solution)/shard_map/all_gather | solution.py:123
  38.6 25.0 %copy-start.20 = (f32[384,768]{1,0:T(8,128)S(1)}, f32[384,768]{1,0:T(8,128)}, u32[]{:S(2)}) copy-start(f32[384,768]{1,0:T(8,128)} %param.32) | copy-start | bytes 3538948
  38.7 218.2 %all-gather.24.cloned.1.call-start = ((), (), s32[]{:S(2)}) async-start(), calls=%async_computation.11 | async-start | bytes 10027008 | tf_op jit(solution)/shard_map/all_gather | solution.py:122
  63.5 356.0 %all-gather.28.cloned.1.call-start = ((), (), s32[]{:S(2)}) async-start(), calls=%async_computation.13 | async-start | bytes 1769472 | tf_op jit(solution)/shard_map/all_gather | solution.py:81
  64.5 357.7 %all-gather.30.cloned.1.call-start = ((), (), s32[]{:S(2)}) async-start(), calls=%async_computation.14 | async-start | bytes 7077888 | tf_op jit(solution)/shard_map/all_gather | solution.py:145
  68.7 369.3 %all-gather.32.cloned.1.call-start = ((), (), s32[]{:S(2)}) async-start(), calls=%async_computation.15 | async-start | bytes 7077888 | tf_op jit(solution)/shard_map/all_gather | solution.py:147
  73.0 10.1 copy-start.48
  73.0 14.5 %copy-start.49 = (f32[384]{0:T(512)S(1)}, f32[384]{0:T(512)}, u32[]{:S(2)}) copy-start(f32[384]{0:T(512)} %param.35) | copy-start | bytes 4612
  73.0 18.9 %copy-start.42 = (f32[1536]{0:T(1024)S(1)}, f32[1536]{0:T(1024)}, u32[]{:S(2)}) copy-start(f32[1536]{0:T(1024)} %param.37) | copy-start | bytes 18436
  73.0 23.3 %copy-start.50 = (f32[384]{0:T(512)S(1)}, f32[384]{0:T(512)}, u32[]{:S(2)}) copy-start(f32[384]{0:T(512)} %param.39) | copy-start | bytes 4612
  73.0 27.8 %copy-start.51 = (f32[384]{0:T(512)S(1)}, f32[384]{0:T(512)}, u32[]{:S(2)}) copy-start(f32[384]{0:T(512)} %param.40) | copy-start | bytes 4612
  73.0 32.2 %copy-start.52 = (f32[384]{0:T(512)S(1)}, f32[384]{0:T(512)}, u32[]{:S(2)}) copy-start(f32[384]{0:T(512)} %param.41) | copy-start | bytes 4612
  73.1 838.0 %reduce-scatter.25.cloned.1.call-start = ((), (), s32[]{:S(2)}) async-start(), calls=%async_computation.19 | async-start | bytes 10027008 | tf_op jit(solution)/shard_map/reshape | solution.py:236
  87.5 368.4 %copy-start.35 = (f32[768]{0:T(1024)}, f32[768]{0:T(1024)S(1)}, u32[]{:S(2)}) copy-start(f32[768]{0:T(1024)S(1)} %reshape.391) | copy-start | bytes 9220
  91.9 346.1 %copy-start.43 = (f32[768]{0:T(1024)}, f32[768]{0:T(1024)S(1)}, u32[]{:S(2)}) copy-start(f32[768]{0:T(1024)S(1)} %reshape.392) | copy-start | bytes 9220
  421.9 34.0 %copy-start.11 = (f32[384,768]{1,0:T(8,128)}, f32[384,768]{1,0:T(8,128)S(1)}, u32[]{:S(2)}) copy-start(f32[384,768]{1,0:T(8,128)S(1)} %get-tuple-element.736) | copy-start | bytes 3538948
  421.9 34.0 %copy-start.33 = (f32[384]{0:T(512)}, f32[384]{0:T(512)S(1)}, u32[]{:S(2)}) copy-start(f32[384]{0:T(512)S(1)} %broadcast_multiply_fusion.1) | copy-start | bytes 4612
  422.2 33.7 %copy-start.37 = (f32[384]{0:T(512)}, f32[384]{0:T(512)S(1)}, u32[]{:S(2)}) copy-start(f32[384]{0:T(512)S(1)} %fusion.98) | copy-start | bytes 4612
  438.0 9.0 copy-start.57
  465.7 9.2 copy-start
  481.5 8.6 copy-start.3
  501.0 9.2 copy-start
  516.7 8.5 copy-start.3
  536.2 9.2 copy-start
  551.9 8.6 copy-start.3
  571.4 9.2 copy-start
  587.2 8.6 copy-start.3
  606.7 9.2 copy-start
  622.4 8.6 copy-start.3
  642.0 9.2 copy-start
  657.6 8.6 copy-start.3
  677.2 9.2 copy-start
  692.9 8.6 copy-start.3
  712.4 9.2 copy-start
  728.2 8.6 copy-start.3
  800.7 225.1 %reduce-scatter.27.cloned.1.call-start = ((), (), s32[]{:S(2)}) async-start(), calls=%async_computation.20 | async-start | bytes 10027008 | tf_op jit(solution)/shard_map/reshape | solution.py:237
  859.9 190.3 %reduce-scatter.29.cloned.1.call-start = ((), (), s32[]{:S(2)}) async-start(), calls=%async_computation.21 | async-start | bytes 1769472
  863.6 211.1 %reduce-scatter.31.cloned.1.call-start = ((), (), s32[]{:S(2)}) async-start(), calls=%async_computation.22 | async-start | bytes 1769472
  914.4 185.0 %reduce-scatter.33.cloned.1.call-start = ((), (), s32[]{:S(2)}) async-start(), calls=%async_computation.23 | async-start | bytes 1769472
  1029.3 94.1 %reduce-scatter.19.cloned.1.call-start = ((), (), s32[]{:S(2)}) async-start(), calls=%async_computation.16 | async-start | bytes 1769472 | tf_op jit(solution)/shard_map/reduce_scatter | solution.py:274
  1031.2 155.1 %reduce-scatter.21.cloned.1.call-start = ((), (), s32[]{:S(2)}) async-start(), calls=%async_computation.17 | async-start | bytes 7077888 | tf_op jit(solution)/shard_map/reduce_scatter | solution.py:286
  1037.5 211.5 %reduce-scatter.23.cloned.1.call-start = ((), (), s32[]{:S(2)}) async-start(), calls=%async_computation.18 | async-start | bytes 7077888 | tf_op jit(solution)/shard_map/reduce_scatter | solution.py:292
  1045.1 360.5 %all-reduce.14.cloned.1.call-start = ((), (), s32[]{:S(2)}) async-start(), calls=%async_computation.24 | async-start | bytes 14155776 | tf_op jit(solution)/shard_map/psum | solution.py:306
  1254.6 78.4 %copy-start.17 = (bf16[768,768]{1,0:T(8,128)(2,1)S(1)}, bf16[768,768]{1,0:T(8,128)(2,1)}, u32[]{:S(2)}) copy-start(bf16[768,768]{1,0:T(8,128)(2,1)} %all-gather.18.cloned.1.call-done) | copy-start | bytes 3538948
  (71 other events, 230.1 us)
Sparse Core Ops, SparseCore 0:
  10.1 25.4 all-gather.17
  37.8 22.7 all-gather.21
  62.7 22.8 all-gather.25
  88.1 83.8 all-gather.19
  174.7 82.0 all-gather.23
  258.8 20.9 all-gather.27
  281.9 62.6 all-gather.29
  346.1 62.6 all-gather.31
  800.9 110.1 reduce-scatter.24
  915.0 110.8 reduce-scatter.26
  1028.7 21.4 reduce-scatter.28
  1052.9 21.8 reduce-scatter.30
  1077.5 21.8 reduce-scatter.32
  1101.5 21.8 reduce-scatter.18
  1126.1 60.0 reduce-scatter.20
  1189.0 60.0 reduce-scatter.22
  1253.9 151.6 all-reduce.13
where the time goes:
time: 1430 us; the launch traced here: 1420 us
  waiting for transfers between devices  605 us (42%)
  matrix products  463 us (32%)
  local copies, waits for them, and re-layouts  176 us (12%)
  blocking collectives  111 us (8%)
  other arithmetic  42 us (3%)
  between operations  16.4 us (1%)
    unnamed x140, local copies, waits for them, and re-layouts  137 us
    reshape x1, waiting for transfers between devices, body(): d_values = value_sum.astype(low_type).reshape(tok_rows, width)  111 us
    all_gather x1, waiting for transfers between devices, body(): lax.all_gather(key_proj, 'ctx', axis=0, tiled=True)  76.2 us
    dot_general x8, matrix products, block_scores(): jnp.einsum('qhd,khd->hqk', d_acc, value_blk, preferred_element_type=jnp.f...  73.6 us
    dot_general x8, matrix products, forward_block(): jnp.einsum('qhd,khd->hqk', query_proj, key_blk, preferred_element_type=jn...  73.1 us
    psum x1, waiting for transfers between devices, body(): lax.psum(shards[0].astype(jnp.bfloat16), 'ctx').astype(jnp.float32)  71 us
    dot_general x8, matrix products, backward_block(): jnp.einsum('hqk,qhd->khd', expo.astype(low_type), d_acc, preferred_elemen...  68.4 us
    dot_general x8, matrix products, forward_block(): jnp.einsum('hqk,khd->qhd', expo.astype(low_type), value_blk, preferred_el...  66 us
  transfers between devices with their start and end apart: 17, of which 13 were waited for; matrix products, arithmetic and copies ran while one was open for 21% of the time, Pallas kernels for 0%

commit v1 on v0

--- a/solution.py
+++ b/solution.py
@@ -7,6 +7,7 @@
 HEADS = 12
 HEAD_DIM = 64
 epsilon = 1e-05
+watch_series_all = lambda unit: lax.all_gather(unit, "ctx").sum(axis=0)
 
 
 def layer_norm(hidden, gain_vec, shift_vec):
@@ -303,7 +304,7 @@
         ).astype(jnp.float32),
     )
     summed = (
-        lax.psum(shards[0].astype(jnp.bfloat16), "ctx").astype(jnp.float32),
+        watch_series_all(shards[0].astype(jnp.bfloat16)).astype(jnp.float32),
         lax.psum(shards[1].astype(jnp.bfloat16), "ctx").astype(jnp.float32),
         lax.psum(shards[2].astype(jnp.bfloat16), "ctx").astype(jnp.float32),
         lax.psum(shards[3].astype(jnp.bfloat16), "ctx").astype(jnp.float32),

time: 1430 us -> 1520 us (1.063)
  waiting for transfers between devices: 605 us -> 672 us
    all_gather x0 -> x1, waiting for transfers between devices: none -> 75.9 us  [watch_series_all = lambda unit: lax.all_gather(unit, 'ctx').sum(axis=0)]
    unnamed x140 -> x139, local copies, waits for them, and re-layouts: 137 us -> 147 us
    unnamed x20 -> x21, waiting for transfers between devices: 50.3 us -> 48.5 us
  transfers between devices with their start and end apart: 17 -> 18, of which waited for: 13 -> 14; matrix products, arithmetic and copies ran while one was open for 21% -> 21% of each run, Pallas kernels for 0% -> 0%
where the time goes in v1:
time: 1520 us; the launch traced here: 1510 us
  waiting for transfers between devices  672 us (44%)
  matrix products  463 us (30%)
  local copies, waits for them, and re-layouts  186 us (12%)
  blocking collectives  111 us (7%)
  other arithmetic  50.2 us (3%)
  between operations  16.9 us (1%)
    unnamed x139, local copies, waits for them, and re-layouts  147 us
    reshape x1, waiting for transfers between devices, body(): d_values = value_sum.astype(low_type).reshape(tok_rows, width)  111 us
    all_gather x1, waiting for transfers between devices, body(): lax.all_gather(key_proj, 'ctx', axis=0, tiled=True)  76.2 us
    all_gather x1, waiting for transfers between devices, watch_series_all = lambda unit: lax.all_gather(unit, 'ctx').sum(axis=0)  75.9 us
    dot_general x8, matrix products, block_scores(): jnp.einsum('qhd,khd->hqk', d_acc, value_blk, preferred_element_type=jnp.f...  73.6 us
    dot_general x8, matrix products, forward_block(): jnp.einsum('qhd,khd->hqk', query_proj, key_blk, preferred_element_type=jn...  73.1 us
    dot_general x8, matrix products, backward_block(): jnp.einsum('hqk,qhd->khd', expo.astype(low_type), d_acc, preferred_elemen...  68.4 us
    dot_general x8, matrix products, forward_block(): jnp.einsum('hqk,khd->qhd', expo.astype(low_type), value_blk, preferred_el...  66 us
  transfers between devices with their start and end apart: 18, of which 14 were waited for; matrix products, arithmetic and copies ran while one was open for 21% of the time, Pallas kernels for 0%

profile of v1, /device:TPU:0, one launch (start us, length us, event | category | flops | bytes accessed | tf_op | source)
XLA Modules:
  0.0 1510.1 jit_solution(6264106471868190424)
XLA Ops:
  16.9 18.7 %all-gather.20.cloned.1.call-done = bf16[768,768]{1,0:T(8,128)(2,1)} async-done(((bf16[384,768]{1,0:T(8,128)(2,1)}), bf16[768,768]{1,0:T(8,128)(2,1)}) %all-gather.20.cloned.1.call-update) | async-done | bytes 1179664 | tf_op jit(solution)/shard_map/all_gather | solution.py:80
  38.7 21.9 %all-gather.24.cloned.1.call-done = bf16[768,768]{1,0:T(8,128)(2,1)} async-done(((bf16[384,768]{1,0:T(8,128)(2,1)}), bf16[768,768]{1,0:T(8,128)(2,1)}) %all-gather.24.cloned.1.call-update) | async-done | bytes 1179664 | tf_op jit(solution)/shard_map/all_gather | solution.py:79
  111.9 60.1 %all-gather.22.cloned.1.call-done = bf16[6144,12,64]{0,2,1:T(8,128)(2,1)} async-done(((bf16[384,12,64]{0,2,1:T(8,128)(2,1)}), bf16[6144,12,64]{0,2,1:T(8,128)(2,1)}) %all-gather.22.cloned.1.call-update) | async-done | bytes 9437200 | tf_op jit(solution)/shard_map/all_gather | solution.py:124
  172.1 8.5 copy.123
  180.6 76.2 %all-gather.26.cloned.1.call-done = bf16[6144,12,64]{0,2,1:T(8,128)(2,1)} async-done(((bf16[384,12,64]{0,2,1:T(8,128)(2,1)}), bf16[6144,12,64]{0,2,1:T(8,128)(2,1)}) %all-gather.26.cloned.1.call-update) | async-done | bytes 9437200 | tf_op jit(solution)/shard_map/all_gather | solution.py:123
  256.8 8.7 copy.122
  265.5 153.1 %while.34 = (s32[]{:T(128)}, f32[384,12,64]{0,2,1:T(8,128)S(1)}, f32[12,384]{1,0:T(8,128)S(1)}, bf16[8,768,12,64]{1,3,2,0:T(8,128)(2,1)}, s32[384]{0:T(512)S(1)}...) while((s32[]{:T(128)}, f32[384,12,64]{0,2,1:T(8,128)S(1)}, ...), condition=%wide.region_7.8_spmd.clone, body=%wide.region_3.7_spmd.clone.sunk | while | flops 921122304 | bytes 34605872 | solution.py:141
  267.4 9.0 fusion.174
  286.2 9.9 fusion.174
  305.9 9.0 fusion.174
  324.6 9.0 fusion.174
  343.4 9.2 fusion.174
  352.6 9.7 fusion.175
  364.0 9.0 fusion.174
  382.8 9.0 fusion.174
  401.5 9.0 fusion.174
  422.3 15.9 %multiply_convert_fusion = (bf16[384,3072]{1,0:T(8,128)(2,1)}, f32[384,3072]{1,0:T(8,128)}, f32[384,3072]{1,0:T(8,128)}) fusion(f32[3072]{0:T(1024)S(1)} %bitcast.229, bf16[768,3072]{1,0:T(8,128)(2,1)} %all-gather.32.cloned.1.call-done, f32[384,768]{1,0:T(8,128)S(1)} %get-tuple-element.735, f32[768]{0:T(1024)S(1)} %reshape.393, f32[768]{0:T(1024)S(1)} %reshape.392, ...), kind=kOutput, calls=%fused_computation.91 | convolution fusion | flops 1891270656 | bytes 17716224 | tf_op jit(solution)/shard_map/dot_general | solution.py:159
  460.3 282.2 %while.35 = (s32[]{:T(128)}, f32[384,12,64]{0,2,1:T(8,128)}, bf16[8,768,12,64]{1,3,2,0:T(8,128)(2,1)}, bf16[8,768,12,64]{1,3,2,0:T(8,128)(2,1)}, bf16[8,768,12,6...) while((s32[]{:T(128)}, f32[384,12,64]{0,2,1:T(8,128)}, ...), condition=%wide.region_20.21_spmd.clone, body=%wide.region_17.20_spmd.clone.sunk | while | flops 2287150080 | bytes 150747632 | solution.py:226
  465.7 9.2 fusion.189
  481.5 8.6 bitcast_dynamic-update-slice_fusion.5
  501.0 9.2 fusion.189
  536.2 9.2 fusion.189
  551.9 8.6 bitcast_dynamic-update-slice_fusion.5
  571.4 9.2 fusion.189
  587.2 8.5 bitcast_dynamic-update-slice_fusion.5
  606.7 9.2 fusion.189
  622.4 8.6 bitcast_dynamic-update-slice_fusion.5
  641.9 9.2 fusion.189
  657.6 8.6 bitcast_dynamic-update-slice_fusion.5
  677.2 9.2 fusion.189
  692.9 8.6 bitcast_dynamic-update-slice_fusion.5
  712.4 9.2 fusion.189
  728.2 8.5 bitcast_dynamic-update-slice_fusion.5
  742.6 28.1 %copy.111 = bf16[8,768,12,64]{3,2,1,0:T(8,128)(2,1)} copy(bf16[8,768,12,64]{1,3,2,0:T(8,128)(2,1)} %get-tuple-element.403) | data formatting | bytes 18874368
  770.7 30.0 %reshape.398 = bf16[6144,768]{1,0:T(8,128)(2,1)} reshape(bf16[6144,12,64]{2,1,0:T(8,128)(2,1)} %bitcast.210) | data formatting | bytes 18874368
  800.8 28.8 %copy.113 = bf16[8,768,12,64]{3,2,1,0:T(8,128)(2,1)} copy(bf16[8,768,12,64]{1,3,2,0:T(8,128)(2,1)} %get-tuple-element.404) | data formatting | bytes 18874368
  829.6 30.3 %reshape.400 = bf16[6144,768]{1,0:T(8,128)(2,1)} reshape(bf16[6144,12,64]{2,1,0:T(8,128)(2,1)} %bitcast.211) | data formatting | bytes 18874368
  860.0 51.0 %reduce-scatter.25.cloned.1.call-done = bf16[384,768]{1,0:T(8,128)(2,1)} async-done(((bf16[6144,768]{1,0:T(8,128)(2,1)}), bf16[384,768]{1,0:T(8,128)(2,1)}) %reduce-scatter.25.cloned.1.call-update) | async-done | bytes 589840 | tf_op jit(solution)/shard_map/reshape | solution.py:237
  914.4 111.4 %reduce-scatter.27.cloned.1.call-done = bf16[384,768]{1,0:T(8,128)(2,1)} async-done(((bf16[6144,768]{1,0:T(8,128)(2,1)}), bf16[384,768]{1,0:T(8,128)(2,1)}) %reduce-scatter.27.cloned.1.call-update) | async-done | bytes 589840 | tf_op jit(solution)/shard_map/reshape | solution.py:238
  1052.3 22.4 %reduce-scatter.33.cloned.1.call-done = bf16[384,768]{1,0:T(8,128)(2,1)} async-done(((bf16[768,768]{1,0:T(8,128)(2,1)}), bf16[384,768]{1,0:T(8,128)(2,1)}) %reduce-scatter.33.cloned.1.call-update) | async-done | bytes 589840
  1076.8 22.0 %reduce-scatter.19.cloned.1.call-done = bf16[384,768]{1,0:T(8,128)(2,1)} async-done(((bf16[768,768]{1,0:T(8,128)(2,1)}), bf16[384,768]{1,0:T(8,128)(2,1)}) %reduce-scatter.19.cloned.1.call-update) | async-done | bytes 589840 | tf_op jit(solution)/shard_map/reduce_scatter | solution.py:275
  1098.8 62.9 %reduce-scatter.21.cloned.1.call-done = bf16[384,3072]{1,0:T(8,128)(2,1)} async-done(((bf16[768,3072]{1,0:T(8,128)(2,1)}), bf16[384,3072]{1,0:T(8,128)(2,1)}) %reduce-scatter.21.cloned.1.call-update) | async-done | bytes 2359312 | tf_op jit(solution)/shard_map/reduce_scatter | solution.py:287
  1161.6 62.8 %reduce-scatter.23.cloned.1.call-done = bf16[1536,768]{1,0:T(8,128)(2,1)} async-done(((bf16[3072,768]{1,0:T(8,128)(2,1)}), bf16[1536,768]{1,0:T(8,128)(2,1)}) %reduce-scatter.23.cloned.1.call-update) | async-done | bytes 2359312 | tf_op jit(solution)/shard_map/reduce_scatter | solution.py:293
  1224.5 24.4 %reduce-scatter.29.cloned.1.call-done = bf16[384,768]{1,0:T(8,128)(2,1)} async-done(((bf16[768,768]{1,0:T(8,128)(2,1)}), bf16[384,768]{1,0:T(8,128)(2,1)}) %reduce-scatter.29.cloned.1.call-update) | async-done | bytes 589840
  1264.9 62.2 %all-reduce.9 = (bf16[384]{0:T(512)(128)(2,1)S(1)}, bf16[384]{0:T(512)(128)(2,1)S(1)}, bf16[384]{0:T(512)(128)(2,1)S(1)}, bf16[384]{0:T(512)(128)(2,1)S(1)}, bf1...) all-reduce(bf16[384]{0:T(512)(128)(2,1)S(1)} %dynamic-slice.1, ...), channel_id=1, replica_groups=mesh['ctx'=16,'wa'=2] {'ctx'}, use_global_device_ids=true, to_apply=%region_27.28 | all-reduce | flops 4608 | bytes 18432 | tf_op jit(solution)/shard_map/psum | solution.py:308
  1336.1 60.8 %all-reduce.14.cloned.1.call-done = (bf16[384,768]{0,1:T(8,128)(2,1)}, bf16[384,768]{0,1:T(8,128)(2,1)}, bf16[384,768]{1,0:T(8,128)(2,1)}, bf16[384,3072]{1,0:T(8,128)(2,1)}, bf16[1536,768]{1,0:T(8,128)(2,1)}) async-done(((bf16[384,768]{0,1:T(8,128)(2,1)}, bf16[384,768]{0,1:T(8,128)(2,1)}, bf16[384,768]{1,0:T(8,128)(2,1)}, bf16[384,3072]{1,0:T(8,128)(2,1)}, bf16[1536,768]{1,0:T(8,128)(2,1)}), ...) | async-done | bytes 6488080 | tf_op jit(solution)/shard_map/psum | solution.py:309
  1407.6 75.9 %all-gather.36.cloned.1.call-done = bf16[6144,768]{0,1:T(8,128)(2,1)} async-done(((bf16[384,768]{0,1:T(8,128)(2,1)}), bf16[6144,768]{0,1:T(8,128)(2,1)}) %all-gather.36.cloned.1.call-update) | async-done | bytes 9437200 | tf_op jit(solution)/shard_map/all_gather | solution.py:10
  1483.5 9.9 copy.119
  (519 shorter events, 372.9 us)
Async XLA Ops:
  7.2 28.4 %all-gather.20.cloned.1.call-start = ((), (), s32[]{:S(2)}) async-start(), calls=%async_computation.8 | async-start | bytes 1769472 | tf_op jit(solution)/shard_map/all_gather | solution.py:80
  9.6 26.1 %copy-start.27 = (bf16[1,384,768]{2,1,0:T(8,128)(2,1)S(1)}, bf16[1,384,768]{2,1,0:T(8,128)(2,1)}, u32[]{:S(2)}) copy-start(bf16[1,384,768]{2,1,0:T(8,128)(2,1)} %param.23) | copy-start | bytes 1769476
  9.6 51.0 %all-gather.24.cloned.1.call-start = ((), (), s32[]{:S(2)}) async-start(), calls=%async_computation.10 | async-start | bytes 1769472 | tf_op jit(solution)/shard_map/all_gather | solution.py:79
  10.6 99.2 %all-gather.28.cloned.1.call-start = ((), (), s32[]{:S(2)}) async-start(), calls=%async_computation.12 | async-start | bytes 1769472 | tf_op jit(solution)/shard_map/all_gather | solution.py:77
  11.5 160.6 %all-gather.22.cloned.1.call-start = ((), (), s32[]{:S(2)}) async-start(), calls=%async_computation.9 | async-start | bytes 10027008 | tf_op jit(solution)/shard_map/all_gather | solution.py:124
  38.6 25.0 %copy-start.20 = (f32[384,768]{1,0:T(8,128)S(1)}, f32[384,768]{1,0:T(8,128)}, u32[]{:S(2)}) copy-start(f32[384,768]{1,0:T(8,128)} %param.32) | copy-start | bytes 3538948
  38.6 218.2 %all-gather.26.cloned.1.call-start = ((), (), s32[]{:S(2)}) async-start(), calls=%async_computation.11 | async-start | bytes 10027008 | tf_op jit(solution)/shard_map/all_gather | solution.py:123
  63.5 356.0 %all-gather.30.cloned.1.call-start = ((), (), s32[]{:S(2)}) async-start(), calls=%async_computation.13 | async-start | bytes 1769472 | tf_op jit(solution)/shard_map/all_gather | solution.py:82
  64.5 357.7 %all-gather.32.cloned.1.call-start = ((), (), s32[]{:S(2)}) async-start(), calls=%async_computation.14 | async-start | bytes 7077888 | tf_op jit(solution)/shard_map/all_gather | solution.py:146
  68.7 369.5 %all-gather.34.cloned.1.call-start = ((), (), s32[]{:S(2)}) async-start(), calls=%async_computation.15 | async-start | bytes 7077888 | tf_op jit(solution)/shard_map/all_gather | solution.py:148
  73.0 10.1 copy-start.47
  73.0 14.5 copy-start.48
  73.0 18.9 %copy-start.41 = (f32[1536]{0:T(1024)S(1)}, f32[1536]{0:T(1024)}, u32[]{:S(2)}) copy-start(f32[1536]{0:T(1024)} %param.37) | copy-start | bytes 18436
  73.0 23.3 %copy-start.49 = (f32[384]{0:T(512)S(1)}, f32[384]{0:T(512)}, u32[]{:S(2)}) copy-start(f32[384]{0:T(512)} %param.39) | copy-start | bytes 4612
  73.0 27.8 %copy-start.50 = (f32[384]{0:T(512)S(1)}, f32[384]{0:T(512)}, u32[]{:S(2)}) copy-start(f32[384]{0:T(512)} %param.40) | copy-start | bytes 4612
  73.0 32.2 %copy-start.51 = (f32[384]{0:T(512)S(1)}, f32[384]{0:T(512)}, u32[]{:S(2)}) copy-start(f32[384]{0:T(512)} %param.41) | copy-start | bytes 4612
  73.1 837.9 %reduce-scatter.25.cloned.1.call-start = ((), (), s32[]{:S(2)}) async-start(), calls=%async_computation.20 | async-start | bytes 10027008 | tf_op jit(solution)/shard_map/reshape | solution.py:237
  87.5 368.6 %copy-start.34 = (f32[768]{0:T(1024)}, f32[768]{0:T(1024)S(1)}, u32[]{:S(2)}) copy-start(f32[768]{0:T(1024)S(1)} %reshape.392) | copy-start | bytes 9220
  91.9 346.3 %copy-start.42 = (f32[768]{0:T(1024)}, f32[768]{0:T(1024)S(1)}, u32[]{:S(2)}) copy-start(f32[768]{0:T(1024)S(1)} %reshape.393) | copy-start | bytes 9220
  421.9 34.2 %copy-start.11 = (f32[384,768]{1,0:T(8,128)}, f32[384,768]{1,0:T(8,128)S(1)}, u32[]{:S(2)}) copy-start(f32[384,768]{1,0:T(8,128)S(1)} %get-tuple-element.735) | copy-start | bytes 3538948
  421.9 34.2 %copy-start.32 = (f32[384]{0:T(512)}, f32[384]{0:T(512)S(1)}, u32[]{:S(2)}) copy-start(f32[384]{0:T(512)S(1)} %broadcast_multiply_fusion.1) | copy-start | bytes 4612
  422.2 33.9 %copy-start.36 = (f32[384]{0:T(512)}, f32[384]{0:T(512)S(1)}, u32[]{:S(2)}) copy-start(f32[384]{0:T(512)S(1)} %fusion.98) | copy-start | bytes 4612
  438.2 9.0 copy-start.56
  465.7 9.2 copy-start
  501.0 9.2 copy-start
  536.2 9.2 copy-start
  571.4 9.2 copy-start
  606.7 9.2 copy-start
  622.4 8.6 copy-start.3
  641.9 9.2 copy-start
  657.6 8.6 copy-start.3
  677.1 9.2 copy-start
  692.9 8.6 copy-start.3
  712.4 9.2 copy-start
  800.7 225.1 %reduce-scatter.27.cloned.1.call-start = ((), (), s32[]{:S(2)}) async-start(), calls=%async_computation.21 | async-start | bytes 10027008 | tf_op jit(solution)/shard_map/reshape | solution.py:238
  859.9 51.1 %copy-start.28 = (bf16[1,384,768]{2,1,0:T(8,128)(2,1)S(1)}, bf16[1,384,768]{2,1,0:T(8,128)(2,1)}, u32[]{:S(2)}) copy-start(bf16[1,384,768]{2,1,0:T(8,128)(2,1)} %param.23) | copy-start | bytes 1769476
  859.9 190.3 %reduce-scatter.31.cloned.1.call-start = ((), (), s32[]{:S(2)}) async-start(), calls=%async_computation.23 | async-start | bytes 1769472
  914.3 160.3 %reduce-scatter.33.cloned.1.call-start = ((), (), s32[]{:S(2)}) async-start(), calls=%async_computation.24 | async-start | bytes 1769472
  1029.2 69.6 %reduce-scatter.19.cloned.1.call-start = ((), (), s32[]{:S(2)}) async-start(), calls=%async_computation.16 | async-start | bytes 1769472 | tf_op jit(solution)/shard_map/reduce_scatter | solution.py:275
  1031.1 130.5 %reduce-scatter.21.cloned.1.call-start = ((), (), s32[]{:S(2)}) async-start(), calls=%async_computation.17 | async-start | bytes 7077888 | tf_op jit(solution)/shard_map/reduce_scatter | solution.py:287
  1037.5 187.0 %reduce-scatter.23.cloned.1.call-start = ((), (), s32[]{:S(2)}) async-start(), calls=%async_computation.18 | async-start | bytes 7077888 | tf_op jit(solution)/shard_map/reduce_scatter | solution.py:293
  1045.0 203.9 %reduce-scatter.29.cloned.1.call-start = ((), (), s32[]{:S(2)}) async-start(), calls=%async_computation.22 | async-start | bytes 1769472
  1048.7 348.1 %all-reduce.14.cloned.1.call-start = ((), (), s32[]{:S(2)}) async-start(), calls=%async_computation.25 | async-start | bytes 12976128 | tf_op jit(solution)/shard_map/psum | solution.py:309
  1224.5 26.7 %copy-start.54 = (u32[32]{0:T(128)S(1)}, u32[32]{0:T(128)}, u32[]{:S(2)}) copy-start(u32[32]{0:T(128)} %constant.320) | copy-start | bytes 388
  1224.5 29.2 %copy-start.8 = (f32[384,768]{1,0:T(8,128)S(1)}, f32[384,768]{1,0:T(8,128)}, u32[]{:S(2)}) copy-start(f32[384,768]{1,0:T(8,128)} %copy-done.7) | copy-start | bytes 3538948
  1224.5 29.2 %copy-start.31 = (f32[384]{0:T(512)S(1)}, f32[384]{0:T(512)}, u32[]{:S(2)}) copy-start(f32[384]{0:T(512)} %copy-done.30) | copy-start | bytes 4612
  1224.5 259.0 %all-gather.36.cloned.1.call-start = ((), (), s32[]{:S(2)}) async-start(), calls=%async_computation.19 | async-start | bytes 10027008 | tf_op jit(solution)/shard_map/all_gather | solution.py:10
  1256.0 78.6 %copy-start.17 = (bf16[768,768]{1,0:T(8,128)(2,1)S(1)}, bf16[768,768]{1,0:T(8,128)(2,1)}, u32[]{:S(2)}) copy-start(bf16[768,768]{1,0:T(8,128)(2,1)} %all-gather.20.cloned.1.call-done) | copy-start | bytes 3538948
  (71 other events, 260.1 us)
Sparse Core Ops, SparseCore 0:
  10.1 25.4 all-gather.19
  37.8 22.7 all-gather.23
  62.7 22.8 all-gather.27
  88.1 83.8 all-gather.21
  174.7 82.0 all-gather.25
  258.8 20.9 all-gather.29
  281.9 62.6 all-gather.31
  346.1 62.6 all-gather.33
  800.8 110.0 reduce-scatter.24
  914.9 110.8 reduce-scatter.26
  1028.6 21.4 reduce-scatter.30
  1052.8 21.8 reduce-scatter.32
  1076.9 21.8 reduce-scatter.18
  1101.5 60.0 reduce-scatter.20
  1164.4 60.0 reduce-scatter.22
  1227.1 21.8 reduce-scatter.28
  1253.7 143.0 all-reduce.13
  1399.4 84.0 all-gather.35
